TPU v7x, 8 devices: a whole 2x2x1 slice. The times are simulated.
8 devices in a mesh: dp: 1 (over z), ep2: 2 (over y), ep: 4 (over x, core).
Axes of the slice: x: 2, y: 2, z: 1, core: 2. Of those that a mesh axis runs over, the one named last changes fastest.
Arguments:
- tokens: bfloat16 [1024, 1536], P(('dp', 'ep2', 'ep'))
- expert_ids: int32 [1024, 8], P(('dp', 'ep2', 'ep'))
- gates: float32 [1024, 8], P(('dp', 'ep2', 'ep'))
- w_gate: bfloat16 [40, 1536, 512], P(('ep2', 'ep'))
- w_up: bfloat16 [40, 1536, 512], P(('ep2', 'ep'))
- w_down: bfloat16 [40, 512, 1536], P(('ep2', 'ep'))
Outputs:
- output: bfloat16 [1024, 1536], P(('dp', 'ep2', 'ep'))
All inputs are finite; a program needn't handle non-finite values.
Results may differ from a plain program's by a relative error of at most 0.001.
Values are sent between devices in bfloat16 or wider.
A program may use at most 1 GiB of HBM per device.

v0:
```python
import jax
import jax.numpy as jnp
from jax import lax
from jax.sharding import PartitionSpec as P


def slot_matrix(expert_ids, n_expert, row_cap):
    n_tok, n_top = expert_ids.shape
    flat_ids = expert_ids.reshape(n_tok * n_top)
    expert_hot = (flat_ids[:, None] == jnp.arange(n_expert)[None, :]).astype(jnp.int32)
    running = jnp.cumsum(expert_hot, axis=0)
    slot_pos = jnp.sum(expert_hot * running, axis=1) - 1
    dest_pos = flat_ids * row_cap + slot_pos
    slot_hot = dest_pos[:, None] == jnp.arange(n_expert * row_cap)[None, :]
    return slot_hot.reshape(n_tok, n_top, n_expert * row_cap).astype(jnp.bfloat16)


def expert_ffn(rows_in, w_gate, w_up, w_down):
    act_gate = jnp.einsum('slcd,ldf->slcf', rows_in, w_gate, preferred_element_type=jnp.float32)
    act_up = jnp.einsum('slcd,ldf->slcf', rows_in, w_up, preferred_element_type=jnp.float32)
    hidden = (jax.nn.silu(act_gate) * act_up).astype(jnp.bfloat16)
    return jnp.einsum('slcf,lfd->slcd', hidden, w_down, preferred_element_type=jnp.float32).astype(jnp.bfloat16)


def solution(mesh):
    group_axes = ('ep2', 'ep')
    n_group = mesh.shape['ep2'] * mesh.shape['ep']
    row_spec = P(('dp', 'ep2', 'ep'), None)
    weight_spec = P(group_axes, None, None)

    def device_step(tokens, expert_ids, gates, w_gate, w_up, w_down):
        n_tok, n_top = expert_ids.shape
        local_count, model_dim = w_gate.shape[0], w_gate.shape[1]
        n_expert = local_count * n_group
        row_cap = -(-(n_tok * n_top) // n_expert)
        slot_hot = slot_matrix(expert_ids, n_expert, row_cap)
        send_buf = jnp.einsum('tjp,td->pd', slot_hot, tokens, preferred_element_type=jnp.float32).astype(jnp.bfloat16)
        recv_buf = lax.all_to_all(send_buf, group_axes, 0, 0, tiled=True)
        expert_out = expert_ffn(recv_buf.reshape(n_group, local_count, row_cap, model_dim), w_gate, w_up, w_down)
        back_buf = lax.all_to_all(expert_out.reshape(n_expert * row_cap, model_dim), group_axes, 0, 0, tiled=True)
        picked = jnp.einsum('tjp,pd->tjd', slot_hot, back_buf, preferred_element_type=jnp.float32)
        total = tokens.astype(jnp.float32)
        for slot_j in range(n_top):
            total = total + gates[:, slot_j:slot_j + 1] * picked[:, slot_j]
        return total.astype(jnp.bfloat16)

    return jax.shard_map(device_step, mesh=mesh, in_specs=(row_spec, row_spec, row_spec, weight_spec, weight_spec, weight_spec), out_specs=row_spec, check_vma=False)
```

profile of v0, /device:TPU:0, one launch (start us, length us, event | category | flops | bytes accessed | tf_op | source)
XLA Modules:
  0.0 141.7 jit_solution(13848700501286676222)
XLA Ops:
  0.0 0.8 copy.44
  0.8 0.1 eq.64
  0.9 0.1 eq.60
  1.0 11.3 %reduce-window.6 = s32[40,8,128]{2,1,0:T(8,128)S(1)} reduce-window(s32[40,8,128]{2,1,0:T(8,128)S(1)} %fusion.51, s32[]{:T(128)} %constant.12.clone.1), window={size=1x1x128 pad=0_0x0_0x127_0}, to_apply=%region_0.0 | reduce-window | flops 5201920 | bytes 327684 | tf_op jit(solution)/shard_map/reduce-window
  12.3 0.1 slice.72
  12.4 0.1 copy.46
  12.5 0.1 copy.47
  12.6 0.1 broadcast_add_fusion
  12.8 0.1 sub.7
  12.9 0.7 multiply_add_fusion
  13.6 0.5 convert_reduce_fusion
  14.2 2.0 %fusion.53 = bf16[1040,1536]{1,0:T(8,128)(2,1)S(1)} fusion(bf16[128,1040]{0,1:T(8,128)(2,1)S(1)} %convert_reduce_fusion, bf16[128,1536]{1,0:T(8,128)(2,1)} %param.6), kind=kOutput, calls=%fused_computation.69 | convolution fusion | flops 408944640 | bytes 3854336 | tf_op jit(solution)/shard_map/tjp,td->pd/dot_general | solution.py:37
  16.2 2.1 %all_to_all.14 = bf16[8,130,1536]{2,1,0:T(8,128)(2,1)} reshape(bf16[1040,1536]{1,0:T(8,128)(2,1)S(1)} %fusion.53) | data formatting | bytes 6389760 | tf_op jit(solution)/shard_map/all_to_all | solution.py:38
  18.3 44.0 %all_to_all.21 = bf16[8,130,1536]{2,1,0:T(8,128)(2,1)S(1)} all-to-all(bf16[8,130,1536]{2,1,0:T(8,128)(2,1)} %all_to_all.14), channel_id=1, replica_groups=mesh['dp'=1,'ep2'=2,'ep'=4] {'ep2','ep'}, dimensions={0} | all-to-all | bytes 6389760 | tf_op jit(solution)/shard_map/all_to_all | solution.py:38
  62.3 1.0 copy.49
  63.2 6.9 %fusion.4 = f32[5,8,26,512]{3,2,1,0:T(8,128)} fusion(bf16[5,1536,512]{2,1,0:T(8,128)(2,1)} %param.9, bf16[8,5,26,1536]{3,0,2,1:T(8,128)(2,1)S(1)} %bitcast.149), kind=kOutput, calls=%fused_computation.4 | convolution fusion | flops 1635778560 | bytes 13189120 | tf_op jit(solution)/shard_map/slcd,ldf->slcf/dot_general | solution.py:19
  70.2 12.7 %fusion.15 = bf16[8,5,26,1536]{3,2,0,1:T(8,128)(2,1)} fusion(bf16[5,512,1536]{2,1,0:T(8,128)(2,1)} %param.11, f32[5,8,26,512]{3,2,1,0:T(8,128)} %fusion.4, bf16[5,1536,512]{2,1,0:T(8,128)(2,1)} %param.10, bf16[8,5,26,1536]{3,0,2,1:T(8,128)(2,1)S(1)} %bitcast.150), kind=kOutput, calls=%fused_computation.16 | convolution fusion | flops 3276349440 | bytes 24248320 | tf_op jit(solution)/shard_map/slcf,lfd->slcd/dot_general | solution.py:22
  82.9 3.9 %copy.52 = bf16[8,5,26,1536]{3,0,2,1:T(8,128)(2,1)S(1)} copy(bf16[8,5,26,1536]{3,2,0,1:T(8,128)(2,1)} %fusion.15) | data formatting | bytes 6389760 | tf_op jit(solution)/shard_map/convert_element_type | solution.py:22
  86.8 2.7 %copy.53 = bf16[8,130,1536]{2,1,0:T(8,128)(2,1)} copy(bf16[8,130,1536]{2,0,1:T(8,128)(2,1)S(1)} %bitcast.148) | data formatting | bytes 6389760 | tf_op jit(solution)/shard_map/all_to_all | solution.py:40
  89.4 0.0 copy-start.1
  89.4 2.7 %all-to-all-start.1 = ((bf16[8,130,1536]{2,1,0:T(8,128)(2,1)}), bf16[8,130,1536]{2,1,0:T(8,128)(2,1)S(1)}, u32[]{:S(2)}, u32[]{:S(2)}) async-start(bf16[8,130,1536]{2,1,0:T(8,128)(2,1)} %copy.53), calls=%async_computation.1 | async-start | bytes 6684672 | tf_op jit(solution)/shard_map/all_to_all | solution.py:40
  92.2 0.0 copy-done.1
  92.2 39.6 %all-to-all-done.1 = bf16[8,130,1536]{2,1,0:T(8,128)(2,1)S(1)} async-done(((bf16[8,130,1536]{2,1,0:T(8,128)(2,1)}), bf16[8,130,1536]{2,1,0:T(8,128)(2,1)S(1)}, u32[]{:S(2)}, u32[]{:S(2)}) %all-to-all-start.1) | async-done | bytes 3194912 | tf_op jit(solution)/shard_map/all_to_all | solution.py:40
  131.8 2.1 %reshape.68 = bf16[1040,1536,1]{1,0,2:T(8,128)(2,1)} reshape(bf16[8,130,1536]{2,1,0:T(8,128)(2,1)S(1)} %all-to-all-done.1) | data formatting | bytes 6389760 | tf_op jit(solution)/shard_map/all_to_all | solution.py:40
  133.9 0.0 copy-start
  133.9 6.5 %fusion.7 = f32[128,8,1536]{2,0,1:T(8,128)S(1)} fusion(bf16[1040,1536,1]{1,0,2:T(8,128)(2,1)} %reshape.68, s32[128,8]{0,1:T(8,128)S(1)} %multiply_add_fusion), kind=kOutput, calls=%fused_computation.11 | convolution fusion | flops 3272622080 | bytes 9490432 | tf_op jit(solution)/shard_map/tjp,pd->tjd/dot_general | solution.py:41
  140.4 0.0 copy-done
  140.4 1.3 fusion.34
  (7 shorter events, 0.1 us)
Async XLA Ops:
  89.4 2.8 %copy-start.1 = (f32[128,8]{0,1:T(8,128)S(1)}, f32[128,8]{0,1:T(8,128)}, u32[]{:S(2)}) copy-start(f32[128,8]{0,1:T(8,128)} %param.8) | copy-start | bytes 12292
  89.4 42.4 %all-to-all-start.1 = ((bf16[8,130,1536]{2,1,0:T(8,128)(2,1)}), bf16[8,130,1536]{2,1,0:T(8,128)(2,1)S(1)}, u32[]{:S(2)}, u32[]{:S(2)}) async-start(bf16[8,130,1536]{2,1,0:T(8,128)(2,1)} %copy.53), calls=%async_computation.1 | async-start | bytes 6684672 | tf_op jit(solution)/shard_map/all_to_all | solution.py:40
  133.9 6.5 %copy-start = (bf16[128,1536]{1,0:T(8,128)(2,1)S(1)}, bf16[128,1536]{1,0:T(8,128)(2,1)}, u32[]{:S(2)}) copy-start(bf16[128,1536]{1,0:T(8,128)(2,1)} %param.6) | copy-start | bytes 1179652
where the time goes:
time: 142 us
  blocking collectives  44 us (31%)
  waiting for transfers between devices  39.6 us (28%)
  matrix products  28 us (20%)
  other arithmetic  14 us (10%)
  local copies, waits for them, and re-layouts  13.1 us (9%)
  starting transfers between devices  2.74 us (2%)
    all_to_all x1, blocking collectives, device_step(): recv_buf = lax.all_to_all(send_buf, group_axes, 0, 0, tiled=True)  44 us
    all_to_all x1, waiting for transfers between devices, device_step(): lax.all_to_all(expert_out.reshape(n_expert * row_cap, model_dim), group_a...  39.6 us
    dot_general x1, matrix products, expert_ffn(): jnp.einsum('slcf,lfd->slcd', hidden, w_down, preferred_element_type=jnp.f...  12.7 us
    another operation x3, other arithmetic  11.4 us
    dot_general x1, matrix products, expert_ffn(): jnp.einsum('slcd,ldf->slcf', rows_in, w_gate, preferred_element_type=jnp....  6.93 us
    dot_general x1, matrix products, device_step(): jnp.einsum('tjp,pd->tjd', slot_hot, back_buf, preferred_element_type=jnp....  6.47 us
    all_to_all x2, local copies, waits for them, and re-layouts, device_step(): lax.all_to_all(expert_out.reshape(n_expert * row_cap, model_dim), group_a...  4.75 us
    convert_element_type x1, local copies, waits for them, and re-layouts, expert_ffn(): jnp.einsum('slcf,lfd->slcd', hidden, w_down, preferred_element_type=jnp.f...  3.9 us
  transfers between devices with their start and end apart: 1, of which 1 were waited for; matrix products, arithmetic and copies ran while one was open for 0% of the time, Pallas kernels for 0%

commit v1 on v0

v1 whole, which is shorter than its diff:
```python
import jax
import jax.numpy as jnp
from jax import lax
from jax.experimental import pallas as pl
from jax.experimental.pallas import tpu as pltpu
from jax.sharding import PartitionSpec as P

MESH = pl.DeviceIdType.MESH
OWN, FIRST, DIAG, SECOND = 0, 1, 2, 3
PAD = 64
BF16_MAX = 3.3895313892515355e38


def split3(v):
    hi = jnp.minimum(v, BF16_MAX).astype(jnp.bfloat16)
    rest = v - hi.astype(jnp.float32)
    mid = rest.astype(jnp.bfloat16)
    low = (rest - mid.astype(jnp.float32)).astype(jnp.bfloat16)
    return hi, mid, low


def layer_kernel(tok_hbm, ids_hbm, gates_hbm, w1_hbm, w3_hbm, w2_hbm, out_ref,
                 xall, meta, ids_v, gates_v, w1, w3, w2, sel, gpart, xs, yb,
                 pmine, pother, qrecv, rbuf,
                 lsem, wsem, msend, mrecv, xsend, xrecv, qsem_s, qsem_r, rsend, rrecv):
    n_local, model, ffn = w1.shape
    n_tok = tok_hbm.shape[0]
    half = model // 2
    dp, y, ep = lax.axis_index("dp"), lax.axis_index("ep2"), lax.axis_index("ep")
    x, c = ep // 2, lax.rem(ep, 2)
    fx, fy = lax.rem(x + 1 - c, 2), lax.rem(y + c, 2)
    sx, sy = lax.rem(x + c, 2), lax.rem(y + 1 - c, 2)
    gx, gy = 1 - x, 1 - y

    def dev(cy, cx, core):
        return (dp, cy, cx * 2 + core)

    partner = dev(y, x, 1 - c)
    first, second, diag = dev(fy, fx, c), dev(sy, sx, c), dev(gy, gx, c)
    first_o, second_o, diag_o = dev(fy, fx, 1 - c), dev(sy, sx, 1 - c), dev(gy, gx, 1 - c)

    cx_own = pltpu.make_async_copy(tok_hbm, xall.at[OWN, 0], lsem.at[0])
    c_ids = pltpu.make_async_copy(ids_hbm, ids_v, lsem.at[1])
    c_gates = pltpu.make_async_copy(gates_hbm, gates_v, lsem.at[2])
    c_ids.start()
    c_gates.start()
    cx_own.start()

    def weight_copies(e):
        return (pltpu.make_async_copy(w1_hbm.at[e], w1.at[e], wsem.at[0, e]),
                pltpu.make_async_copy(w3_hbm.at[e], w3.at[e], wsem.at[1, e]),
                pltpu.make_async_copy(w2_hbm.at[e], w2.at[e], wsem.at[2, e]))

    for e in range(n_local):
        for cp in weight_copies(e):
            cp.start()

    barrier = pltpu.get_barrier_semaphore()
    peers = (partner, first, second, diag, first_o, second_o, diag_o)
    for peer in peers:
        pl.semaphore_signal(barrier, inc=1, device_id=peer, device_id_type=MESH)

    c_ids.wait()
    c_gates.wait()
    eye8 = (lax.broadcasted_iota(jnp.int32, (8, 8), 0)
            == lax.broadcasted_iota(jnp.int32, (8, 8), 1)).astype(jnp.float32).astype(jnp.bfloat16)

    def flip(v):
        return lax.dot_general(eye8, v, (((1,), (1,)), ((), ())), preferred_element_type=jnp.float32)

    g_hi, g_mid, g_low = split3(gates_v[...])
    meta[OWN, 0, 0:8, :] = flip(ids_v[...].astype(jnp.float32).astype(jnp.bfloat16))
    meta[OWN, 0, 8:16, :] = (flip(g_hi) + flip(g_mid)) + flip(g_low)
    yb[n_local * PAD:, :] = jnp.zeros((yb.shape[0] - n_local * PAD, model), jnp.bfloat16)

    pl.semaphore_wait(barrier, 7)

    def remote(src, dst, ssem, rsem, to):
        return pltpu.make_async_remote_copy(src_ref=src, dst_ref=dst, send_sem=ssem, recv_sem=rsem,
                                            device_id=to, device_id_type=MESH)

    meta_to = ((partner, OWN, 1), (first, FIRST, 0), (second, SECOND, 0), (diag, DIAG, 0),
               (diag_o, DIAG, 1), (second_o, SECOND, 1), (first_o, FIRST, 1))
    m_copies = [remote(meta.at[OWN, 0], meta.at[p, s], msend.at[k], mrecv.at[k], to)
                for k, (to, p, s) in enumerate(meta_to)]
    for cp in m_copies:
        cp.start()
    meta_of = {(p, s): m_copies[k] for k, (to, p, s) in enumerate(meta_to)}

    x_own_partner = remote(xall.at[OWN, 0], xall.at[OWN, 1], xsend.at[0], xrecv.at[0], partner)
    x_first = remote(xall.at[OWN, 0], xall.at[FIRST, 0], xsend.at[1], xrecv.at[1], first)
    x_second = remote(xall.at[OWN, 0], xall.at[SECOND, 0], xsend.at[2], xrecv.at[2], second)
    x_diag = remote(xall.at[FIRST, 0], xall.at[DIAG, 0], xsend.at[3], xrecv.at[3], second)
    x_fwd = {p: remote(xall.at[p, 0], xall.at[p, 1], xsend.at[3 + p], xrecv.at[3 + p], partner)
             for p in (FIRST, DIAG, SECOND)}

    cx_own.wait()
    x_first.start()
    x_own_partner.start()

    base = ((y * 4 + ep) * n_local).astype(jnp.float32)

    def route(p):
        ids = jnp.concatenate([meta[p, 0, 0:8, :], meta[p, 1, 0:8, :]], axis=1)
        gts = jnp.concatenate([meta[p, 0, 8:16, :], meta[p, 1, 8:16, :]], axis=1)
        n2 = 2 * n_tok
        chosen, gate = [], []
        for e in range(n_local):
            hit = ids == base + float(e)
            chosen.append(jnp.sum(jnp.where(hit, 1.0, 0.0), axis=0, keepdims=True))
            gate.append(jnp.sum(jnp.where(hit, gts, 0.0), axis=0, keepdims=True))
        chosen8 = jnp.concatenate(chosen + [jnp.zeros((8 - n_local, n2), jnp.float32)], axis=0)
        upper = (lax.broadcasted_iota(jnp.int32, (n2, n2), 0)
                 < lax.broadcasted_iota(jnp.int32, (n2, n2), 1)).astype(jnp.float32).astype(jnp.bfloat16)
        rank = jnp.dot(chosen8.astype(jnp.bfloat16), upper, preferred_element_type=jnp.float32)
        pos = jnp.where(chosen8 > 0.0, rank, 999.0)
        slot = lax.broadcasted_iota(jnp.int32, (PAD, n2), 0).astype(jnp.float32)
        rows = []
        for e in range(n_local):
            mask = pos[e:e + 1, :] == slot
            sel[e * PAD:(e + 1) * PAD, :] = jnp.where(mask, 1.0, 0.0).astype(jnp.bfloat16)
            rows.append(jnp.where(mask, gate[e], 0.0))
        rows.append(jnp.zeros((yb.shape[0] - n_local * PAD, n2), jnp.float32))
        spread = jnp.concatenate(rows, axis=0).T
        for k, piece in enumerate(split3(spread)):
            gpart[k] = piece

    def gather(p):
        for k in range(3):
            cols = pl.ds(k * (model // 3), model // 3)
            xg = xall[p, :, :, cols].reshape(2 * n_tok, model // 3)
            xs[:, cols] = jnp.dot(sel[...], xg, preferred_element_type=jnp.float32).astype(jnp.bfloat16)

    def ffn(fresh):
        def step(e, carry):
            if fresh:
                for cp in weight_copies(e):
                    cp.wait()
            rows = pl.ds(pl.multiple_of(e * PAD, PAD), PAD)
            xr = xs[rows, :]
            a = jnp.dot(xr, w1[e], preferred_element_type=jnp.float32)
            b = jnp.dot(xr, w3[e], preferred_element_type=jnp.float32)
            h = (jax.nn.silu(a) * b).astype(jnp.bfloat16)
            yb[rows, :] = jnp.dot(h, w2[e], preferred_element_type=jnp.float32).astype(jnp.bfloat16)
            return carry
        lax.fori_loop(0, n_local, step, 0)

    q_copies = {(p, h): remote(pother.at[p, h], qrecv.at[p, h], qsem_s.at[2 * p + h], qsem_r.at[2 * p + h], partner)
                for p in range(4) for h in range(2)}

    def combine(p):
        for h in range(2):
            ycols = yb[:, h * half:(h + 1) * half]
            acc = jnp.dot(gpart[2], ycols, preferred_element_type=jnp.float32)
            acc = acc + jnp.dot(gpart[1], ycols, preferred_element_type=jnp.float32)
            acc = acc + jnp.dot(gpart[0], ycols, preferred_element_type=jnp.float32)
            pmine[p, h] = acc[:n_tok]
            pother[p, h] = acc[n_tok:]
            q_copies[p, h].start()

    def chip_sum(p, h):
        q_copies[p, h].wait_recv()
        pmine[p, h] = pmine[p, h] + qrecv[p, h]

    r_copies = []

    def send(src, slot, rows, to):
        k = len(r_copies)
        view = slice(None) if rows is None else pl.ds(*rows)
        cp = remote(src.at[view], rbuf.at[slot].at[view], rsend.at[k], rrecv.at[k], to)
        r_copies.append(cp)
        cp.start()
        return cp

    hr = n_tok // 2

    meta_of[OWN, 1].wait_recv()
    route(OWN)
    x_own_partner.wait_recv()
    gather(OWN)
    ffn(True)
    combine(OWN)

    x_first.wait_recv()
    x_fwd[FIRST].start()
    x_diag.start()
    x_second.start()
    meta_of[FIRST, 0].wait_recv()
    meta_of[FIRST, 1].wait_recv()
    route(FIRST)
    x_fwd[FIRST].wait_recv()
    gather(FIRST)
    ffn(False)
    combine(FIRST)

    x_diag.wait_recv()
    x_fwd[DIAG].start()
    meta_of[DIAG, 0].wait_recv()
    meta_of[DIAG, 1].wait_recv()
    route(DIAG)
    chip_sum(FIRST, 0)
    to_first = send(pmine.at[FIRST, 0], 0, None, first)
    chip_sum(FIRST, 1)
    x_fwd[DIAG].wait_recv()
    gather(DIAG)
    ffn(False)
    combine(DIAG)

    x_second.wait_recv()
    x_fwd[SECOND].start()
    meta_of[SECOND, 0].wait_recv()
    meta_of[SECOND, 1].wait_recv()
    route(SECOND)
    chip_sum(DIAG, 0)
    d_first = [send(pmine.at[DIAG, 0], 2, (k * hr, hr), first) for k in range(2)]
    chip_sum(DIAG, 1)
    d_second = [send(pmine.at[DIAG, 1], 3, (k * hr, hr), second) for k in range(2)]
    x_fwd[SECOND].wait_recv()
    gather(SECOND)
    ffn(False)
    combine(SECOND)

    chip_sum(OWN, 0)
    chip_sum(OWN, 1)
    chip_sum(SECOND, 1)
    to_second = send(pmine.at[SECOND, 1], 1, None, second)
    chip_sum(SECOND, 0)

    tail = []
    for k in range(2):
        rows = pl.ds(k * hr, hr)
        d_second[k].wait_recv()
        pmine[FIRST, 1, rows, :] = pmine[FIRST, 1, rows, :] + rbuf[3, rows, :]
        tail.append(send(pmine.at[FIRST, 1], 5, (k * hr, hr), first))
        d_first[k].wait_recv()
        pmine[SECOND, 0, rows, :] = pmine[SECOND, 0, rows, :] + rbuf[2, rows, :]
        tail.append(send(pmine.at[SECOND, 0], 4, (k * hr, hr), second))

    to_first.wait_recv()
    to_second.wait_recv()
    for h in range(2):
        cols = pl.ds(h * half, half)
        pmine[OWN, h] = (pmine[OWN, h] + xall[OWN, 0, :, cols].astype(jnp.float32)) + rbuf[h]
    for k in range(2):
        rows = pl.ds(k * hr, hr)
        tail[2 * k].wait_recv()
        out_ref[rows, half:] = (pmine[OWN, 1, rows, :] + rbuf[5, rows, :]).astype(jnp.bfloat16)
        tail[2 * k + 1].wait_recv()
        out_ref[rows, :half] = (pmine[OWN, 0, rows, :] + rbuf[4, rows, :]).astype(jnp.bfloat16)

    for cp in m_copies + [x_own_partner, x_first, x_second, x_diag] + list(x_fwd.values()) + list(q_copies.values()) + r_copies:
        cp.wait_send()


def solution(mesh):
    row_spec = P(('dp', 'ep2', 'ep'), None)
    weight_spec = P(('ep2', 'ep'), None, None)

    def device_step(tokens, expert_ids, gates, w_gate, w_up, w_down):
        n_tok, model = tokens.shape
        n_local, _, ffn = w_gate.shape
        n_top = expert_ids.shape[1]
        half = model // 2
        bf16, f32 = jnp.bfloat16, jnp.float32
        dma = pltpu.SemaphoreType.DMA
        any_spec = pl.BlockSpec(memory_space=pl.ANY)
        return pl.pallas_call(
            layer_kernel,
            out_shape=jax.ShapeDtypeStruct((n_tok, model), bf16),
            in_specs=[any_spec] * 6,
            out_specs=pl.BlockSpec(memory_space=pltpu.VMEM),
            scratch_shapes=[
                pltpu.VMEM((4, 2, n_tok, model), bf16),
                pltpu.VMEM((4, 2, 16, n_tok), f32),
                pltpu.VMEM((n_tok, n_top), jnp.int32),
                pltpu.VMEM((n_tok, n_top), f32),
                pltpu.VMEM((n_local, model, ffn), bf16),
                pltpu.VMEM((n_local, model, ffn), bf16),
                pltpu.VMEM((n_local, ffn, model), bf16),
                pltpu.VMEM((n_local * PAD, 2 * n_tok), bf16),
                pltpu.VMEM((3, 2 * n_tok, 6 * PAD), bf16),
                pltpu.VMEM((n_local * PAD, model), bf16),
                pltpu.VMEM((6 * PAD, model), bf16),
                pltpu.VMEM((4, 2, n_tok, half), f32),
                pltpu.VMEM((4, 2, n_tok, half), f32),
                pltpu.VMEM((4, 2, n_tok, half), f32),
                pltpu.VMEM((6, n_tok, half), f32),
                dma((3,)),
                dma((3, n_local)),
                dma((7,)), dma((7,)),
                dma((7,)), dma((7,)),
                dma((8,)), dma((8,)),
                dma((10,)), dma((10,)),
            ],
            compiler_params=pltpu.CompilerParams(
                collective_id=0, has_side_effects=True, vmem_limit_bytes=60 * 1024 * 1024),
        )(tokens, expert_ids, gates, w_gate, w_up, w_down)

    return jax.shard_map(device_step, mesh=mesh, in_specs=(row_spec, row_spec, row_spec, weight_spec, weight_spec, weight_spec), out_specs=row_spec, check_vma=False)
```

time: 142 us -> 72 us (0.51)
  Pallas kernels: 0 us -> 67.2 us
  blocking collectives: 44 us -> 0 us
  waiting for transfers between devices: 39.6 us -> 0 us
  matrix products: 28 us -> 0 us
  other arithmetic: 14 us -> 0 us
  local copies, waits for them, and re-layouts: 13.1 us -> 4.59 us
  starting transfers between devices: 2.74 us -> 0 us
    pallas_call x0 -> x1, Pallas kernels: none -> 67.2 us  [device_step(): pl.pallas_call(layer_kernel, out_shape=jax.ShapeDtypeStruct((n_tok, model...]
    all_to_all x1 -> x0, blocking collectives: 44 us -> none  [device_step(): recv_buf = lax.all_to_all(send_buf, group_axes, 0, 0, tiled=True)]
    all_to_all x1 -> x0, waiting for transfers between devices: 39.6 us -> none  [device_step(): lax.all_to_all(expert_out.reshape(n_expert * row_cap, model_dim), group_a...]
    dot_general x4 -> x0, matrix products: 28 us -> none  [the longest x1 12.7 us: expert_ffn(): jnp.einsum('slcf,lfd->slcd', hidden, w_down, preferred_element_type=jnp.f...]
    another operation x3 -> x0, other arithmetic: 11.4 us -> none
    all_to_all x4 -> x0, local copies, waits for them, and re-layouts: 7.83 us -> none  [the longest x2 4.75 us: device_step(): lax.all_to_all(expert_out.reshape(n_expert * row_cap, model_dim), group_a...]
    convert_element_type x1 -> x0, local copies, waits for them, and re-layouts: 3.9 us -> none  [expert_ffn(): jnp.einsum('slcf,lfd->slcd', hidden, w_down, preferred_element_type=jnp.f...]
    unnamed x5 -> x3, local copies, waits for them, and re-layouts: 0.79 us -> 4.59 us
  transfers between devices with their start and end apart: 1 -> 0, of which waited for: 1 -> 0; matrix products, arithmetic and copies ran while one was open for 0% -> 0% of each run, Pallas kernels for 0% -> 0%
where the time goes in v1:
time: 72 us; the launch traced here: 71.8 us
  Pallas kernels  67.2 us (93%)
  local copies, waits for them, and re-layouts  4.59 us (6%)
    pallas_call x1, Pallas kernels, device_step(): pl.pallas_call(layer_kernel, out_shape=jax.ShapeDtypeStruct((n_tok, model...  67.2 us
    unnamed x3, local copies, waits for them, and re-layouts  4.59 us

profile of v1, /device:TPU:0, one launch (start us, length us, event | category | flops | bytes accessed | tf_op | source)
XLA Modules:
  0.0 71.8 jit_solution(17277994852100852685)
XLA Ops:
  0.0 1.4 %copy.7.ids_hbm = s32[128,8]{1,0:T(8,128)} copy(s32[128,8]{0,1:T(8,128)} %param.7) | data formatting | bytes 8192 | tf_op args[1]
  1.4 1.4 %copy.8.gates_hbm = f32[128,8]{1,0:T(8,128)} copy(f32[128,8]{0,1:T(8,128)} %param.8) | data formatting | bytes 8192 | tf_op args[2]
  2.8 67.2 %shard_map.64 = bf16[128,1536]{1,0:T(8,128)(2,1)} custom-call(bf16[128,1536]{1,0:T(8,128)(2,1)} %tok_hbm.1, s32[128,8]{1,0:T(8,128)} %copy.7.ids_hbm, f32[128,8]{1,0:T(8,128)} %copy.8.gates_hbm, bf16[5,1536,512]{2,1,0:T(8,128)(2,1)} %w1_hbm.1, bf16[5,1536,512]{2,1,0:T(8,128)(2,1)} %w3_hbm.1, bf16[5,512,1536]{2,1,0:T(8,128)(2,1)} %w2_hbm.1), custom_call_target="tpu_custom_call" | custom-call | tf_op jit(solution)/shard_map/pallas_call | solution.py:267
  70.1 1.8 %copy.10 = bf16[128,1536]{1,0:T(8,128)(2,1)} copy(bf16[128,1536]{1,0:T(8,128)(2,1)} %shard_map.64) | data formatting | bytes 786432

commit v2 on v0

v2 whole, which is shorter than its diff:
```python
import jax
import jax.numpy as jnp
from jax import lax
from jax.experimental import pallas as pl
from jax.experimental.pallas import tpu as pltpu
from jax.sharding import PartitionSpec as P

MESH = pl.DeviceIdType.MESH
OWN, FIRST, DIAG, SECOND = 0, 1, 2, 3
PAD, RANKS = 64, 32
BF16_MAX = 3.3895313892515355e38


def split3(v):
    hi = jnp.minimum(v, BF16_MAX).astype(jnp.bfloat16)
    rest = v - hi.astype(jnp.float32)
    mid = rest.astype(jnp.bfloat16)
    low = (rest - mid.astype(jnp.float32)).astype(jnp.bfloat16)
    return hi, mid, low


def layer_kernel(tok_hbm, ids_hbm, gates_hbm, w1_hbm, w3_hbm, w2_hbm, out_hbm,
                 xall, meta, ids_v, w1, w3, w2, sel, gpart, xs, yb,
                 pmine, pother, qrecv, rbuf, out_v,
                 lsem, wsem, osem, msend, mrecv, xsend, xrecv, qsem_s, qsem_r, rsend, rrecv):
    n_local, model, ffn_dim = w1.shape
    n_tok = tok_hbm.shape[0]
    half, hr = model // 2, n_tok // 2
    dp, y, ep = lax.axis_index("dp"), lax.axis_index("ep2"), lax.axis_index("ep")
    x, c = ep // 2, lax.rem(ep, 2)
    fx, fy = lax.rem(x + 1 - c, 2), lax.rem(y + c, 2)
    sx, sy = lax.rem(x + c, 2), lax.rem(y + 1 - c, 2)

    def dev(cy, cx, core):
        return (dp, cy, cx * 2 + core)

    partner, first, second = dev(y, x, 1 - c), dev(fy, fx, c), dev(sy, sx, c)

    c_ids = pltpu.make_async_copy(ids_hbm, ids_v, lsem.at[1])
    c_gates = pltpu.make_async_copy(gates_hbm, meta.at[OWN, 0, pl.ds(8, 8)], lsem.at[2])
    c_own = pltpu.make_async_copy(tok_hbm, xall.at[OWN, 0], lsem.at[0])
    c_ids.start()
    c_gates.start()
    c_own.start()

    barrier = pltpu.get_barrier_semaphore()
    for peer in (partner, first, second):
        pl.semaphore_signal(barrier, inc=1, device_id=peer, device_id_type=MESH)

    def weight_copies(e):
        return (pltpu.make_async_copy(w1_hbm.at[e], w1.at[e], wsem.at[0, e]),
                pltpu.make_async_copy(w3_hbm.at[e], w3.at[e], wsem.at[1, e]),
                pltpu.make_async_copy(w2_hbm.at[e], w2.at[e], wsem.at[2, e]))

    for e in range(n_local):
        for cp in weight_copies(e):
            cp.start()

    c_ids.wait()
    meta[OWN, 0, 0:8, :] = ids_v[...].astype(jnp.float32)
    c_gates.wait()
    c_own.wait()

    def remote(src, dst, ssem, rsem, to):
        return pltpu.make_async_remote_copy(src_ref=src, dst_ref=dst, send_sem=ssem, recv_sem=rsem,
                                            device_id=to, device_id_type=MESH)

    hops = ((OWN, OWN, 1, partner), (OWN, FIRST, 0, first), (OWN, SECOND, 0, second), (FIRST, DIAG, 0, second),
            (FIRST, FIRST, 1, partner), (DIAG, DIAG, 1, partner), (SECOND, SECOND, 1, partner))
    m_hop = [remote(meta.at[s, 0], meta.at[p, q], msend.at[k], mrecv.at[k], to)
             for k, (s, p, q, to) in enumerate(hops)]
    x_hop = {k: remote(xall.at[s, 0], xall.at[p, q], xsend.at[k], xrecv.at[k], to)
             for k, (s, p, q, to) in enumerate(hops) if k != 2}
    second_cut = [remote(xall.at[OWN, 0, pl.ds(k * hr, hr)], xall.at[SECOND, 0, pl.ds(k * hr, hr)],
                         xsend.at[(2, 7)[k]], xrecv.at[(2, 7)[k]], second) for k in range(2)]

    pl.semaphore_wait(barrier, 3)
    m_hop[1].start()
    x_hop[1].start()
    m_hop[0].start()
    x_hop[0].start()
    m_hop[2].start()
    yb[:, :, n_local * RANKS:, :] = jnp.zeros((2, 2, yb.shape[2] - n_local * RANKS, model), jnp.bfloat16)

    base = ((y * 4 + ep) * n_local).astype(jnp.float32)

    def route(p, b):
        n2 = 2 * n_tok
        ids = jnp.concatenate([meta[p, 0, 0:8, :], meta[p, 1, 0:8, :]], axis=1)
        gts = jnp.concatenate([meta[p, 0, 8:16, :], meta[p, 1, 8:16, :]], axis=1)
        chosen, gate = [], []
        for e in range(n_local):
            hit = ids == base + float(e)
            chosen.append(jnp.sum(jnp.where(hit, 1.0, 0.0), axis=0, keepdims=True))
            gate.append(jnp.sum(jnp.where(hit, gts, 0.0), axis=0, keepdims=True))
        chosen8 = jnp.concatenate(chosen + [jnp.zeros((8 - n_local, n2), jnp.float32)], axis=0)
        row, col = lax.broadcasted_iota(jnp.int32, (n2, n2), 0), lax.broadcasted_iota(jnp.int32, (n2, n2), 1)
        earlier = ((row < col) & ((row < n_tok) == (col < n_tok))).astype(jnp.float32).astype(jnp.bfloat16)
        rank = jnp.dot(chosen8.astype(jnp.bfloat16), earlier, preferred_element_type=jnp.float32)
        pos = jnp.where(chosen8 > 0.0, rank, 999.0)
        slot = lax.broadcasted_iota(jnp.int32, (RANKS, n_tok), 0).astype(jnp.float32)
        none = jnp.zeros((RANKS, n_tok), jnp.bfloat16)
        for q in range(2):
            lanes = slice(q * n_tok, (q + 1) * n_tok)
            rows = []
            for e in range(n_local):
                mask = pos[e:e + 1, lanes] == slot
                at = e * PAD + q * RANKS
                sel[at:at + RANKS, lanes] = jnp.where(mask, 1.0, 0.0).astype(jnp.bfloat16)
                sel[at:at + RANKS, (1 - q) * n_tok:(2 - q) * n_tok] = none
                rows.append(jnp.where(mask, gate[e][:, lanes], 0.0))
            rows.append(jnp.zeros((yb.shape[2] - n_local * RANKS, n_tok), jnp.float32))
            spread = jnp.concatenate(rows, axis=0).T
            for k, piece in enumerate(split3(spread)):
                gpart[b, q, k] = piece

    def gather(p):
        for k in range(3):
            cols = pl.ds(k * (model // 3), model // 3)
            xg = xall[p, :, :, cols].reshape(2 * n_tok, model // 3)
            xs[:, cols] = jnp.dot(sel[...], xg, preferred_element_type=jnp.float32).astype(jnp.bfloat16)

    def ffn(b, fresh=False, hooks={}):
        for e in range(n_local):
            for hook in hooks.get(e, ()):
                hook()
            if fresh:
                for cp in weight_copies(e):
                    cp.wait()
            xr = xs[e * PAD:(e + 1) * PAD, :]
            up = jnp.dot(xr, w1[e], preferred_element_type=jnp.float32)
            lin = jnp.dot(xr, w3[e], preferred_element_type=jnp.float32)
            h = (jax.nn.silu(up) * lin).astype(jnp.bfloat16)
            yr = jnp.dot(h, w2[e], preferred_element_type=jnp.float32).astype(jnp.bfloat16)
            for q in range(2):
                yb[b, q, e * RANKS:(e + 1) * RANKS, :] = yr[q * RANKS:(q + 1) * RANKS]

    q_copies = {(p, h): remote(pother.at[p, h], qrecv.at[p, h], qsem_s.at[2 * p + h], qsem_r.at[2 * p + h], partner)
                for p in range(4) for h in range(2)}

    def combine(p, b, h):
        for q in (1, 0):
            ycols = yb[b, q, :, h * half:(h + 1) * half]
            acc = jnp.dot(gpart[b, q, 2], ycols, preferred_element_type=jnp.float32)
            acc = acc + jnp.dot(gpart[b, q, 1], ycols, preferred_element_type=jnp.float32)
            acc = acc + jnp.dot(gpart[b, q, 0], ycols, preferred_element_type=jnp.float32)
            if q == 1:
                pother[p, h] = acc
                q_copies[p, h].start()
            else:
                pmine[p, h] = acc

    def chip_sum(p, h):
        q_copies[p, h].wait_recv()
        pmine[p, h] = pmine[p, h] + qrecv[p, h]

    returns = {"to_first": (FIRST, 0, 0, first), "to_second": (SECOND, 1, 1, second),
               "diag_first": (DIAG, 0, 2, first), "diag_second": (DIAG, 1, 3, second),
               "last_second": (SECOND, 0, 4, second), "last_first": (FIRST, 1, 5, first)}
    ret = {name: [remote(pmine.at[p, h, pl.ds(k * hr, hr)], rbuf.at[slot, pl.ds(k * hr, hr)],
                         rsend.at[slot, k], rrecv.at[slot, k], to) for k in range(2)]
           for name, (p, h, slot, to) in returns.items()}

    def start_both(name):
        for cp in ret[name]:
            cp.start()

    def sum_and_send(p, h, name):
        def run():
            chip_sum(p, h)
            start_both(name)
        return run

    def on_first_sent():
        x_hop[1].wait_send()
        second_cut[0].start()

    def on_first():
        m_hop[1].wait_recv()
        m_hop[4].start()
        m_hop[3].start()
        x_hop[1].wait_recv()
        x_hop[4].start()
        x_hop[3].start()
        second_cut[1].start()

    def on_diag():
        m_hop[3].wait_recv()
        m_hop[5].start()
        x_hop[3].wait_recv()
        x_hop[5].start()

    def on_second():
        m_hop[2].wait_recv()
        m_hop[6].start()
        for cp in second_cut:
            cp.wait_recv()
        x_hop[6].start()

    m_hop[0].wait_recv()
    route(OWN, 1)
    x_hop[0].wait_recv()
    gather(OWN)
    ffn(1, True, {3: (on_first_sent,), 4: (on_first,)})

    m_hop[4].wait_recv()
    route(FIRST, 0)
    x_hop[4].wait_recv()
    gather(FIRST)
    ffn(0)
    combine(FIRST, 0, 0)
    on_diag()
    combine(FIRST, 0, 1)

    m_hop[5].wait_recv()
    route(DIAG, 0)
    sum_and_send(FIRST, 0, "to_first")()
    x_hop[5].wait_recv()
    gather(DIAG)
    ffn(0, False, {1: (on_second,), 2: (lambda: chip_sum(FIRST, 1),)})
    combine(DIAG, 0, 0)
    combine(DIAG, 0, 1)

    m_hop[6].wait_recv()
    route(SECOND, 0)
    x_hop[6].wait_recv()
    gather(SECOND)
    ffn(0, False, {1: (sum_and_send(DIAG, 0, "diag_first"),), 2: (sum_and_send(DIAG, 1, "diag_second"),)})
    combine(SECOND, 0, 1)
    combine(SECOND, 0, 0)
    combine(OWN, 1, 0)
    sum_and_send(SECOND, 1, "to_second")()
    combine(OWN, 1, 1)
    chip_sum(SECOND, 0)

    for k in range(2):
        rows = pl.ds(k * hr, hr)
        ret["diag_second"][k].wait_recv()
        pmine[FIRST, 1, rows, :] = pmine[FIRST, 1, rows, :] + rbuf[3, rows, :]
        ret["last_first"][k].start()
        ret["diag_first"][k].wait_recv()
        pmine[SECOND, 0, rows, :] = pmine[SECOND, 0, rows, :] + rbuf[2, rows, :]
        ret["last_second"][k].start()
    chip_sum(OWN, 0)
    chip_sum(OWN, 1)
    for h, name in ((0, "to_first"), (1, "to_second")):
        for cp in ret[name]:
            cp.wait_recv()
        cols = pl.ds(h * half, half)
        pmine[OWN, h] = (pmine[OWN, h] + xall[OWN, 0, :, cols].astype(jnp.float32)) + rbuf[h]
    outs = []
    for k in range(2):
        rows = pl.ds(k * hr, hr)
        ret["last_first"][k].wait_recv()
        out_v[rows, half:] = (pmine[OWN, 1, rows, :] + rbuf[5, rows, :]).astype(jnp.bfloat16)
        ret["last_second"][k].wait_recv()
        out_v[rows, :half] = (pmine[OWN, 0, rows, :] + rbuf[4, rows, :]).astype(jnp.bfloat16)
        outs.append(pltpu.make_async_copy(out_v.at[rows], out_hbm.at[rows], osem.at[k]))
        outs[-1].start()

    for cp in m_hop + [x_hop[k] for k in (0, 3, 4, 5, 6)] + second_cut + list(q_copies.values()):
        cp.wait_send()
    for pair in ret.values():
        for cp in pair:
            cp.wait_send()
    for cp in outs:
        cp.wait()


def solution(mesh):
    row_spec = P(('dp', 'ep2', 'ep'), None)
    weight_spec = P(('ep2', 'ep'), None, None)

    def device_step(tokens, expert_ids, gates, w_gate, w_up, w_down):
        n_tok, model = tokens.shape
        n_local, _, ffn = w_gate.shape
        n_top = expert_ids.shape[1]
        half = model // 2
        bf16, f32 = jnp.bfloat16, jnp.float32
        dma = pltpu.SemaphoreType.DMA
        any_spec = pl.BlockSpec(memory_space=pl.ANY)
        return pl.pallas_call(
            layer_kernel,
            out_shape=jax.ShapeDtypeStruct((n_tok, model), bf16),
            in_specs=[any_spec] * 6,
            out_specs=any_spec,
            scratch_shapes=[
                pltpu.VMEM((4, 2, n_tok, model), bf16),
                pltpu.VMEM((4, 2, 16, n_tok), f32),
                pltpu.VMEM((n_top, n_tok), jnp.int32),
                pltpu.VMEM((n_local, model, ffn), bf16),
                pltpu.VMEM((n_local, model, ffn), bf16),
                pltpu.VMEM((n_local, ffn, model), bf16),
                pltpu.VMEM((n_local * PAD, 2 * n_tok), bf16),
                pltpu.VMEM((2, 2, 3, n_tok, 8 * RANKS), bf16),
                pltpu.VMEM((n_local * PAD, model), bf16),
                pltpu.VMEM((2, 2, 8 * RANKS, model), bf16),
                pltpu.VMEM((4, 2, n_tok, half), f32),
                pltpu.VMEM((4, 2, n_tok, half), f32),
                pltpu.VMEM((4, 2, n_tok, half), f32),
                pltpu.VMEM((6, n_tok, half), f32),
                pltpu.VMEM((n_tok, model), bf16),
                dma((3,)), dma((3, n_local)), dma((2,)),
                dma((7,)), dma((7,)),
                dma((8,)), dma((8,)),
                dma((8,)), dma((8,)),
                dma((6, 2)), dma((6, 2)),
            ],
            compiler_params=pltpu.CompilerParams(
                collective_id=0, has_side_effects=True, vmem_limit_bytes=60 * 1024 * 1024),
        )(tokens, expert_ids.T, gates.T, w_gate, w_up, w_down)

    return jax.shard_map(device_step, mesh=mesh, in_specs=(row_spec, row_spec, row_spec, weight_spec, weight_spec, weight_spec), out_specs=row_spec, check_vma=False)
```

time: 142 us -> 53.8 us (0.38)
  Pallas kernels: 0 us -> 51.9 us
  blocking collectives: 44 us -> 0 us
  waiting for transfers between devices: 39.6 us -> 0 us
  matrix products: 28 us -> 0 us
  other arithmetic: 14 us -> 0 us
  local copies, waits for them, and re-layouts: 13.1 us -> 1.77 us
  starting transfers between devices: 2.74 us -> 0 us
    pallas_call x0 -> x1, Pallas kernels: none -> 51.9 us  [device_step(): pl.pallas_call(layer_kernel, out_shape=jax.ShapeDtypeStruct((n_tok, model...]
    all_to_all x1 -> x0, blocking collectives: 44 us -> none  [device_step(): recv_buf = lax.all_to_all(send_buf, group_axes, 0, 0, tiled=True)]
    all_to_all x1 -> x0, waiting for transfers between devices: 39.6 us -> none  [device_step(): lax.all_to_all(expert_out.reshape(n_expert * row_cap, model_dim), group_a...]
    dot_general x4 -> x0, matrix products: 28 us -> none  [the longest x1 12.7 us: expert_ffn(): jnp.einsum('slcf,lfd->slcd', hidden, w_down, preferred_element_type=jnp.f...]
    another operation x3 -> x0, other arithmetic: 11.4 us -> none
    all_to_all x4 -> x0, local copies, waits for them, and re-layouts: 7.83 us -> none  [the longest x2 4.75 us: device_step(): lax.all_to_all(expert_out.reshape(n_expert * row_cap, model_dim), group_a...]
    convert_element_type x1 -> x0, local copies, waits for them, and re-layouts: 3.9 us -> none  [expert_ffn(): jnp.einsum('slcf,lfd->slcd', hidden, w_down, preferred_element_type=jnp.f...]
    all_to_all x1 -> x0, starting transfers between devices: 2.74 us -> none  [device_step(): lax.all_to_all(expert_out.reshape(n_expert * row_cap, model_dim), group_a...]
  transfers between devices with their start and end apart: 1 -> 0, of which waited for: 1 -> 0; matrix products, arithmetic and copies ran while one was open for 0% -> 0% of each run, Pallas kernels for 0% -> 0%
where the time goes in v2:
time: 53.8 us; the launch traced here: 53.7 us
  Pallas kernels  51.9 us (96%)
  local copies, waits for them, and re-layouts  1.77 us (3%)
    pallas_call x1, Pallas kernels, device_step(): pl.pallas_call(layer_kernel, out_shape=jax.ShapeDtypeStruct((n_tok, model...  51.9 us
    unnamed x1, local copies, waits for them, and re-layouts  1.77 us

profile of v2, /device:TPU:0, one launch (start us, length us, event | category | flops | bytes accessed | tf_op | source)
XLA Modules:
  0.0 53.7 jit_solution(8240885238609815699)
XLA Ops:
  0.0 51.9 %shard_map.64 = bf16[128,1536]{1,0:T(8,128)(2,1)} custom-call(bf16[128,1536]{1,0:T(8,128)(2,1)} %tok_hbm.1, s32[8,128]{1,0:T(8,128)} %bitcast.2, f32[8,128]{1,0:T(8,128)} %bitcast.3, bf16[5,1536,512]{2,1,0:T(8,128)(2,1)} %w1_hbm.1, bf16[5,1536,512]{2,1,0:T(8,128)(2,1)} %w3_hbm.1, bf16[5,512,1536]{2,1,0:T(8,128)(2,1)} %w2_hbm.1), custom_call_target="tpu_custom_call" | custom-call | tf_op jit(solution)/shard_map/pallas_call | solution.py:282
  51.9 1.8 %copy.8 = bf16[128,1536]{1,0:T(8,128)(2,1)} copy(bf16[128,1536]{1,0:T(8,128)(2,1)} %shard_map.64) | data formatting | bytes 786432

commit v3 on v2

--- a/solution.py
+++ b/solution.py
@@ -7,7 +7,7 @@
 
 MESH = pl.DeviceIdType.MESH
 OWN, FIRST, DIAG, SECOND = 0, 1, 2, 3
-PAD, RANKS = 64, 32
+PAD, RANKS, CUTS = 64, 32, 4
 BF16_MAX = 3.3895313892515355e38
 
 
@@ -69,17 +69,26 @@
             (FIRST, FIRST, 1, partner), (DIAG, DIAG, 1, partner), (SECOND, SECOND, 1, partner))
     m_hop = [remote(meta.at[s, 0], meta.at[p, q], msend.at[k], mrecv.at[k], to)
              for k, (s, p, q, to) in enumerate(hops)]
-    x_hop = {k: remote(xall.at[s, 0], xall.at[p, q], xsend.at[k], xrecv.at[k], to)
-             for k, (s, p, q, to) in enumerate(hops) if k != 2}
-    second_cut = [remote(xall.at[OWN, 0, pl.ds(k * hr, hr)], xall.at[SECOND, 0, pl.ds(k * hr, hr)],
-                         xsend.at[(2, 7)[k]], xrecv.at[(2, 7)[k]], second) for k in range(2)]
+    cut = n_tok // CUTS
+    x_hop = [[remote(xall.at[s, 0, pl.ds(i * cut, cut)], xall.at[p, q, pl.ds(i * cut, cut)],
+                     xsend.at[k, i], xrecv.at[k, i], to) for i in range(CUTS)]
+             for k, (s, p, q, to) in enumerate(hops)]
+
+    def start_x(k):
+        for cp in x_hop[k]:
+            cp.start()
+
+    def wait_x(k):
+        for cp in x_hop[k]:
+            cp.wait_recv()
 
     pl.semaphore_wait(barrier, 3)
     m_hop[1].start()
-    x_hop[1].start()
+    start_x(1)
     m_hop[0].start()
-    x_hop[0].start()
+    start_x(0)
     m_hop[2].start()
+    xs[n_local * PAD:, :] = jnp.zeros((PAD, model), jnp.bfloat16)
     yb[:, :, n_local * RANKS:, :] = jnp.zeros((2, 2, yb.shape[2] - n_local * RANKS, model), jnp.bfloat16)
 
     base = ((y * 4 + ep) * n_local).astype(jnp.float32)
@@ -118,22 +127,36 @@
         for k in range(3):
             cols = pl.ds(k * (model // 3), model // 3)
             xg = xall[p, :, :, cols].reshape(2 * n_tok, model // 3)
-            xs[:, cols] = jnp.dot(sel[...], xg, preferred_element_type=jnp.float32).astype(jnp.bfloat16)
+            xs[:n_local * PAD, cols] = jnp.dot(sel[...], xg, preferred_element_type=jnp.float32).astype(jnp.bfloat16)
+
+    def up(e):
+        xr = xs[e * PAD:e * PAD + 2 * PAD, :]
+        act = jnp.dot(xr, w1[e], preferred_element_type=jnp.float32)
+        lin = jnp.dot(xr, w3[e], preferred_element_type=jnp.float32)
+        return (jax.nn.silu(act) * lin).astype(jnp.bfloat16)
+
+    def down(e, b, h):
+        yr = jnp.dot(h, w2[e], preferred_element_type=jnp.float32)
+        for q in range(2):
+            yb[b, q, e * RANKS:(e + 1) * RANKS, :] = yr[q * RANKS:(q + 1) * RANKS].astype(jnp.bfloat16)
 
     def ffn(b, fresh=False, hooks={}):
-        for e in range(n_local):
-            for hook in hooks.get(e, ()):
-                hook()
+        def ready(e):
             if fresh:
                 for cp in weight_copies(e):
                     cp.wait()
-            xr = xs[e * PAD:(e + 1) * PAD, :]
-            up = jnp.dot(xr, w1[e], preferred_element_type=jnp.float32)
-            lin = jnp.dot(xr, w3[e], preferred_element_type=jnp.float32)
-            h = (jax.nn.silu(up) * lin).astype(jnp.bfloat16)
-            yr = jnp.dot(h, w2[e], preferred_element_type=jnp.float32).astype(jnp.bfloat16)
-            for q in range(2):
-                yb[b, q, e * RANKS:(e + 1) * RANKS, :] = yr[q * RANKS:(q + 1) * RANKS]
+            return up(e)
+
+        h = None if fresh else up(0)
+        for e in range(n_local):
+            if fresh:
+                h, ahead = ready(e), None
+            else:
+                ahead = up(e + 1) if e + 1 < n_local else None
+            down(e, b, h)
+            h = ahead
+            for hook in hooks.get(e, ()):
+                hook()
 
     q_copies = {(p, h): remote(pother.at[p, h], qrecv.at[p, h], qsem_s.at[2 * p + h], qsem_r.at[2 * p + h], partner)
                 for p in range(4) for h in range(2)}
@@ -171,61 +194,61 @@
             start_both(name)
         return run
 
-    def on_first_sent():
-        x_hop[1].wait_send()
-        second_cut[0].start()
-
-    def on_first():
-        m_hop[1].wait_recv()
-        m_hop[4].start()
-        m_hop[3].start()
-        x_hop[1].wait_recv()
-        x_hop[4].start()
-        x_hop[3].start()
-        second_cut[1].start()
-
-    def on_diag():
-        m_hop[3].wait_recv()
-        m_hop[5].start()
-        x_hop[3].wait_recv()
-        x_hop[5].start()
+    def on_first(i):
+        if i == 0:
+            m_hop[1].wait_recv()
+            m_hop[4].start()
+            m_hop[3].start()
+        x_hop[1][i].wait_recv()
+        x_hop[3][i].start()
+        x_hop[4][i].start()
+
+    def on_diag(i):
+        if i == 0:
+            m_hop[3].wait_recv()
+            m_hop[5].start()
+        x_hop[3][i].wait_recv()
+        x_hop[5][i].start()
 
     def on_second():
         m_hop[2].wait_recv()
         m_hop[6].start()
-        for cp in second_cut:
-            cp.wait_recv()
-        x_hop[6].start()
+        wait_x(2)
+        start_x(6)
+
+    def after_three():
+        on_first(2)
+        m_hop[4].wait_recv()
+        route(FIRST, 0)
+        on_first(3)
+        start_x(2)
 
     m_hop[0].wait_recv()
     route(OWN, 1)
-    x_hop[0].wait_recv()
+    wait_x(0)
     gather(OWN)
-    ffn(1, True, {3: (on_first_sent,), 4: (on_first,)})
-
-    m_hop[4].wait_recv()
-    route(FIRST, 0)
-    x_hop[4].wait_recv()
+    ffn(1, True, {1: (lambda: on_first(0),), 2: (lambda: on_first(1),), 3: (after_three,)})
+
+    wait_x(4)
     gather(FIRST)
-    ffn(0)
+    ffn(0, False, {3: (lambda: on_diag(0), lambda: on_diag(1), lambda: on_diag(2)), 4: (lambda: on_diag(3),)})
     combine(FIRST, 0, 0)
-    on_diag()
     combine(FIRST, 0, 1)
 
     m_hop[5].wait_recv()
     route(DIAG, 0)
-    sum_and_send(FIRST, 0, "to_first")()
-    x_hop[5].wait_recv()
+    wait_x(5)
     gather(DIAG)
-    ffn(0, False, {1: (on_second,), 2: (lambda: chip_sum(FIRST, 1),)})
+    ffn(0, False, {0: (sum_and_send(FIRST, 0, "to_first"),), 2: (lambda: chip_sum(FIRST, 1),), 3: (on_second,)})
     combine(DIAG, 0, 0)
     combine(DIAG, 0, 1)
 
     m_hop[6].wait_recv()
     route(SECOND, 0)
-    x_hop[6].wait_recv()
+    wait_x(6)
     gather(SECOND)
-    ffn(0, False, {1: (sum_and_send(DIAG, 0, "diag_first"),), 2: (sum_and_send(DIAG, 1, "diag_second"),)})
+    ffn(0, False, {0: (sum_and_send(DIAG, 0, "diag_first"),), 1: (sum_and_send(DIAG, 1, "diag_second"),),
+                   })
     combine(SECOND, 0, 1)
     combine(SECOND, 0, 0)
     combine(OWN, 1, 0)
@@ -258,7 +281,7 @@
         outs.append(pltpu.make_async_copy(out_v.at[rows], out_hbm.at[rows], osem.at[k]))
         outs[-1].start()
 
-    for cp in m_hop + [x_hop[k] for k in (0, 3, 4, 5, 6)] + second_cut + list(q_copies.values()):
+    for cp in m_hop + [cp for pair in x_hop for cp in pair] + list(q_copies.values()):
         cp.wait_send()
     for pair in ret.values():
         for cp in pair:
@@ -293,7 +316,7 @@
                 pltpu.VMEM((n_local, ffn, model), bf16),
                 pltpu.VMEM((n_local * PAD, 2 * n_tok), bf16),
                 pltpu.VMEM((2, 2, 3, n_tok, 8 * RANKS), bf16),
-                pltpu.VMEM((n_local * PAD, model), bf16),
+                pltpu.VMEM(((n_local + 1) * PAD, model), bf16),
                 pltpu.VMEM((2, 2, 8 * RANKS, model), bf16),
                 pltpu.VMEM((4, 2, n_tok, half), f32),
                 pltpu.VMEM((4, 2, n_tok, half), f32),
@@ -302,7 +325,7 @@
                 pltpu.VMEM((n_tok, model), bf16),
                 dma((3,)), dma((3, n_local)), dma((2,)),
                 dma((7,)), dma((7,)),
-                dma((8,)), dma((8,)),
+                dma((7, CUTS)), dma((7, CUTS)),
                 dma((8,)), dma((8,)),
                 dma((6, 2)), dma((6, 2)),
             ],

time: 53.8 us -> 51.5 us (0.957)
  Pallas kernels: 51.9 us -> 49.6 us
    pallas_call x1, Pallas kernels: 51.9 us -> 49.6 us  [device_step(): pl.pallas_call(layer_kernel, out_shape=jax.ShapeDtypeStruct((n_tok, model...]
where the time goes in v3:
time: 51.5 us; the launch traced here: 51.4 us
  Pallas kernels  49.6 us (96%)
  local copies, waits for them, and re-layouts  1.77 us (3%)
    pallas_call x1, Pallas kernels, device_step(): pl.pallas_call(layer_kernel, out_shape=jax.ShapeDtypeStruct((n_tok, model...  49.6 us
    unnamed x1, local copies, waits for them, and re-layouts  1.77 us

profile of v3, /device:TPU:0, one launch (start us, length us, event | category | flops | bytes accessed | tf_op | source)
XLA Modules:
  0.0 51.4 jit_solution(6172877006102457762)
XLA Ops:
  0.0 49.6 %shard_map.64 = bf16[128,1536]{1,0:T(8,128)(2,1)} custom-call(bf16[128,1536]{1,0:T(8,128)(2,1)} %tok_hbm.1, s32[8,128]{1,0:T(8,128)} %bitcast.2, f32[8,128]{1,0:T(8,128)} %bitcast.3, bf16[5,1536,512]{2,1,0:T(8,128)(2,1)} %w1_hbm.1, bf16[5,1536,512]{2,1,0:T(8,128)(2,1)} %w3_hbm.1, bf16[5,512,1536]{2,1,0:T(8,128)(2,1)} %w2_hbm.1), custom_call_target="tpu_custom_call" | custom-call | tf_op jit(solution)/shard_map/pallas_call | solution.py:305
  49.6 1.8 %copy.8 = bf16[128,1536]{1,0:T(8,128)(2,1)} copy(bf16[128,1536]{1,0:T(8,128)(2,1)} %shard_map.64) | data formatting | bytes 786432

commit v4 on v3

--- a/solution.py
+++ b/solution.py
@@ -19,10 +19,10 @@
     return hi, mid, low
 
 
-def layer_kernel(tok_hbm, ids_hbm, gates_hbm, w1_hbm, w3_hbm, w2_hbm, out_hbm,
+def layer_kernel(tok_hbm, ids_hbm, gates_hbm, w1_hbm, w3_hbm, w2_hbm, out_ref,
                  xall, meta, ids_v, w1, w3, w2, sel, gpart, xs, yb,
-                 pmine, pother, qrecv, rbuf, out_v,
-                 lsem, wsem, osem, msend, mrecv, xsend, xrecv, qsem_s, qsem_r, rsend, rrecv):
+                 pmine, pother, qrecv, rbuf,
+                 lsem, wsem, msend, mrecv, xsend, xrecv, qsem_s, qsem_r, rsend, rrecv):
     n_local, model, ffn_dim = w1.shape
     n_tok = tok_hbm.shape[0]
     half, hr = model // 2, n_tok // 2
@@ -239,16 +239,18 @@
     route(DIAG, 0)
     wait_x(5)
     gather(DIAG)
-    ffn(0, False, {0: (sum_and_send(FIRST, 0, "to_first"),), 2: (lambda: chip_sum(FIRST, 1),), 3: (on_second,)})
+    ffn(0, False, {0: (sum_and_send(FIRST, 0, "to_first"),), 2: (lambda: chip_sum(FIRST, 1),)})
     combine(DIAG, 0, 0)
     combine(DIAG, 0, 1)
 
+    on_second()
     m_hop[6].wait_recv()
     route(SECOND, 0)
+    sum_and_send(DIAG, 0, "diag_first")()
+    sum_and_send(DIAG, 1, "diag_second")()
     wait_x(6)
     gather(SECOND)
-    ffn(0, False, {0: (sum_and_send(DIAG, 0, "diag_first"),), 1: (sum_and_send(DIAG, 1, "diag_second"),),
-                   })
+    ffn(0)
     combine(SECOND, 0, 1)
     combine(SECOND, 0, 0)
     combine(OWN, 1, 0)
@@ -271,23 +273,17 @@
             cp.wait_recv()
         cols = pl.ds(h * half, half)
         pmine[OWN, h] = (pmine[OWN, h] + xall[OWN, 0, :, cols].astype(jnp.float32)) + rbuf[h]
-    outs = []
     for k in range(2):
         rows = pl.ds(k * hr, hr)
         ret["last_first"][k].wait_recv()
-        out_v[rows, half:] = (pmine[OWN, 1, rows, :] + rbuf[5, rows, :]).astype(jnp.bfloat16)
+        out_ref[rows, half:] = (pmine[OWN, 1, rows, :] + rbuf[5, rows, :]).astype(jnp.bfloat16)
         ret["last_second"][k].wait_recv()
-        out_v[rows, :half] = (pmine[OWN, 0, rows, :] + rbuf[4, rows, :]).astype(jnp.bfloat16)
-        outs.append(pltpu.make_async_copy(out_v.at[rows], out_hbm.at[rows], osem.at[k]))
-        outs[-1].start()
-
+        out_ref[rows, :half] = (pmine[OWN, 0, rows, :] + rbuf[4, rows, :]).astype(jnp.bfloat16)
     for cp in m_hop + [cp for pair in x_hop for cp in pair] + list(q_copies.values()):
         cp.wait_send()
     for pair in ret.values():
         for cp in pair:
             cp.wait_send()
-    for cp in outs:
-        cp.wait()
 
 
 def solution(mesh):
@@ -304,9 +300,9 @@
         any_spec = pl.BlockSpec(memory_space=pl.ANY)
         return pl.pallas_call(
             layer_kernel,
-            out_shape=jax.ShapeDtypeStruct((n_tok, model), bf16),
+            out_shape=pltpu.MemorySpace.VMEM((n_tok, model), bf16),
             in_specs=[any_spec] * 6,
-            out_specs=any_spec,
+            out_specs=pl.BlockSpec(memory_space=pltpu.VMEM),
             scratch_shapes=[
                 pltpu.VMEM((4, 2, n_tok, model), bf16),
                 pltpu.VMEM((4, 2, 16, n_tok), f32),
@@ -322,8 +318,7 @@
                 pltpu.VMEM((4, 2, n_tok, half), f32),
                 pltpu.VMEM((4, 2, n_tok, half), f32),
                 pltpu.VMEM((6, n_tok, half), f32),
-                pltpu.VMEM((n_tok, model), bf16),
-                dma((3,)), dma((3, n_local)), dma((2,)),
+                dma((3,)), dma((3, n_local)),
                 dma((7,)), dma((7,)),
                 dma((7, CUTS)), dma((7, CUTS)),
                 dma((8,)), dma((8,)),

time: 51.5 us -> 49.8 us (0.967)
  local copies, waits for them, and re-layouts: 1.77 us -> 0.75 us
  Pallas kernels: 49.6 us -> 48.9 us
    unnamed x1, local copies, waits for them, and re-layouts: 1.77 us -> 0.75 us
    pallas_call x1, Pallas kernels: 49.6 us -> 48.9 us  [device_step(): pl.pallas_call(layer_kernel, out_shape=pltpu.MemorySpace.VMEM((n_tok, mod...]
where the time goes in v4:
time: 49.8 us; the launch traced here: 49.7 us
  Pallas kernels  48.9 us (98%)
  local copies, waits for them, and re-layouts  0.75 us (2%)
    pallas_call x1, Pallas kernels, device_step(): pl.pallas_call(layer_kernel, out_shape=pltpu.MemorySpace.VMEM((n_tok, mod...  48.9 us

profile of v4, /device:TPU:0, one launch (start us, length us, event | category | flops | bytes accessed | tf_op | source)
XLA Modules:
  0.0 49.7 jit_solution(12616801073982528779)
XLA Ops:
  0.0 48.9 %shard_map.64 = bf16[128,1536]{1,0:T(8,128)(2,1)S(1)} custom-call(bf16[128,1536]{1,0:T(8,128)(2,1)} %tok_hbm.1, s32[8,128]{1,0:T(8,128)} %bitcast.2, f32[8,128]{1,0:T(8,128)} %bitcast.3, bf16[5,1536,512]{2,1,0:T(8,128)(2,1)} %w1_hbm.1, bf16[5,1536,512]{2,1,0:T(8,128)(2,1)} %w3_hbm.1, bf16[5,512,1536]{2,1,0:T(8,128)(2,1)} %w2_hbm.1), custom_call_target="tpu_custom_call" | custom-call | tf_op jit(solution)/shard_map/pallas_call | solution.py:301
  48.9 0.7 %copy.8 = bf16[128,1536]{1,0:T(8,128)(2,1)} copy(bf16[128,1536]{1,0:T(8,128)(2,1)S(1)} %shard_map.64) | data formatting | bytes 786432

commit v5 on v4

--- a/solution.py
+++ b/solution.py
@@ -200,8 +200,17 @@
             m_hop[4].start()
             m_hop[3].start()
         x_hop[1][i].wait_recv()
-        x_hop[3][i].start()
         x_hop[4][i].start()
+        if i < CUTS - 1:
+            @pl.when(c == 0)
+            def _():
+                x_hop[3][i].start()
+        if i > 0:
+            @pl.when(c == 1)
+            def _():
+                x_hop[3][i - 1].start()
+        if i == CUTS - 1:
+            x_hop[3][i].start()
 
     def on_diag(i):
         if i == 0:
@@ -231,7 +240,7 @@
 
     wait_x(4)
     gather(FIRST)
-    ffn(0, False, {3: (lambda: on_diag(0), lambda: on_diag(1), lambda: on_diag(2)), 4: (lambda: on_diag(3),)})
+    ffn(0, False, {2: (lambda: on_diag(0), lambda: on_diag(1),), 3: (lambda: on_diag(2), lambda: on_diag(3),)})
     combine(FIRST, 0, 0)
     combine(FIRST, 0, 1)
 

time: 49.8 us -> 49.1 us (0.986)
  Pallas kernels: 48.9 us -> 48.3 us
    pallas_call x1, Pallas kernels: 48.9 us -> 48.3 us  [device_step(): pl.pallas_call(layer_kernel, out_shape=pltpu.MemorySpace.VMEM((n_tok, mod...]
where the time goes in v5:
time: 49.1 us; the launch traced here: 49 us
  Pallas kernels  48.3 us (98%)
  local copies, waits for them, and re-layouts  0.75 us (2%)
    pallas_call x1, Pallas kernels, device_step(): pl.pallas_call(layer_kernel, out_shape=pltpu.MemorySpace.VMEM((n_tok, mod...  48.3 us

profile of v5, /device:TPU:0, one launch (start us, length us, event | category | flops | bytes accessed | tf_op | source)
XLA Modules:
  0.0 49.0 jit_solution(10597322641898002825)
XLA Ops:
  0.0 48.3 %shard_map.64 = bf16[128,1536]{1,0:T(8,128)(2,1)S(1)} custom-call(bf16[128,1536]{1,0:T(8,128)(2,1)} %tok_hbm.1, s32[8,128]{1,0:T(8,128)} %bitcast.2, f32[8,128]{1,0:T(8,128)} %bitcast.3, bf16[5,1536,512]{2,1,0:T(8,128)(2,1)} %w1_hbm.1, bf16[5,1536,512]{2,1,0:T(8,128)(2,1)} %w3_hbm.1, bf16[5,512,1536]{2,1,0:T(8,128)(2,1)} %w2_hbm.1), custom_call_target="tpu_custom_call" | custom-call | tf_op jit(solution)/shard_map/pallas_call | solution.py:310
  48.3 0.7 %copy.8 = bf16[128,1536]{1,0:T(8,128)(2,1)} copy(bf16[128,1536]{1,0:T(8,128)(2,1)S(1)} %shard_map.64) | data formatting | bytes 786432

commit v6 on v5

--- a/solution.py
+++ b/solution.py
@@ -89,7 +89,7 @@
     start_x(0)
     m_hop[2].start()
     xs[n_local * PAD:, :] = jnp.zeros((PAD, model), jnp.bfloat16)
-    yb[:, :, n_local * RANKS:, :] = jnp.zeros((2, 2, yb.shape[2] - n_local * RANKS, model), jnp.bfloat16)
+    yb[:, :, n_local * RANKS:, :] = jnp.zeros((3, 2, yb.shape[2] - n_local * RANKS, model), jnp.bfloat16)
 
     base = ((y * 4 + ep) * n_local).astype(jnp.float32)
 
@@ -242,15 +242,15 @@
     gather(FIRST)
     ffn(0, False, {2: (lambda: on_diag(0), lambda: on_diag(1),), 3: (lambda: on_diag(2), lambda: on_diag(3),)})
     combine(FIRST, 0, 0)
-    combine(FIRST, 0, 1)
 
     m_hop[5].wait_recv()
-    route(DIAG, 0)
+    route(DIAG, 2)
     wait_x(5)
     gather(DIAG)
-    ffn(0, False, {0: (sum_and_send(FIRST, 0, "to_first"),), 2: (lambda: chip_sum(FIRST, 1),)})
-    combine(DIAG, 0, 0)
-    combine(DIAG, 0, 1)
+    ffn(2, False, {0: (sum_and_send(FIRST, 0, "to_first"),)})
+    combine(DIAG, 2, 0)
+    combine(DIAG, 2, 1)
+    combine(FIRST, 0, 1)
 
     on_second()
     m_hop[6].wait_recv()
@@ -259,7 +259,7 @@
     sum_and_send(DIAG, 1, "diag_second")()
     wait_x(6)
     gather(SECOND)
-    ffn(0)
+    ffn(0, False, {1: (lambda: chip_sum(FIRST, 1),)})
     combine(SECOND, 0, 1)
     combine(SECOND, 0, 0)
     combine(OWN, 1, 0)
@@ -320,9 +320,9 @@
                 pltpu.VMEM((n_local, model, ffn), bf16),
                 pltpu.VMEM((n_local, ffn, model), bf16),
                 pltpu.VMEM((n_local * PAD, 2 * n_tok), bf16),
-                pltpu.VMEM((2, 2, 3, n_tok, 8 * RANKS), bf16),
+                pltpu.VMEM((3, 2, 3, n_tok, 8 * RANKS), bf16),
                 pltpu.VMEM(((n_local + 1) * PAD, model), bf16),
-                pltpu.VMEM((2, 2, 8 * RANKS, model), bf16),
+                pltpu.VMEM((3, 2, 8 * RANKS, model), bf16),
                 pltpu.VMEM((4, 2, n_tok, half), f32),
                 pltpu.VMEM((4, 2, n_tok, half), f32),
                 pltpu.VMEM((4, 2, n_tok, half), f32),

time: 49.1 us -> 49 us (level)
  no operation moved by 1% of the time
where the time goes in v6:
time: 49 us; the launch traced here: 48.8 us
  Pallas kernels  48.1 us (98%)
  local copies, waits for them, and re-layouts  0.75 us (2%)
    pallas_call x1, Pallas kernels, device_step(): pl.pallas_call(layer_kernel, out_shape=pltpu.MemorySpace.VMEM((n_tok, mod...  48.1 us

profile of v6, /device:TPU:0, one launch (start us, length us, event | category | flops | bytes accessed | tf_op | source)
XLA Modules:
  0.0 48.8 jit_solution(3572605693189142077)
XLA Ops:
  0.0 48.1 %shard_map.64 = bf16[128,1536]{1,0:T(8,128)(2,1)S(1)} custom-call(bf16[128,1536]{1,0:T(8,128)(2,1)} %tok_hbm.1, s32[8,128]{1,0:T(8,128)} %bitcast.2, f32[8,128]{1,0:T(8,128)} %bitcast.3, bf16[5,1536,512]{2,1,0:T(8,128)(2,1)} %w1_hbm.1, bf16[5,1536,512]{2,1,0:T(8,128)(2,1)} %w3_hbm.1, bf16[5,512,1536]{2,1,0:T(8,128)(2,1)} %w2_hbm.1), custom_call_target="tpu_custom_call" | custom-call | tf_op jit(solution)/shard_map/pallas_call | solution.py:310
  48.1 0.7 %copy.8 = bf16[128,1536]{1,0:T(8,128)(2,1)} copy(bf16[128,1536]{1,0:T(8,128)(2,1)S(1)} %shard_map.64) | data formatting | bytes 786432
